TPU v7x, 32 devices: a whole 2x2x4 slice. The times are simulated.
32 devices in a mesh: lat: 4 (over x, core), lon: 8 (over z, y).
Axes of the slice: x: 2, y: 2, z: 4, core: 2. Of those that a mesh axis runs over, the one named last changes fastest.
Arguments:
- prediction_fields: float32 [4, 69, 360, 512], P(None, None, 'lon', 'lat'), may hold values from -16 to 16
- verifying_state: float32 [69, 360, 512], P(None, 'lon', 'lat'), may hold values from -16 to 16
- normal_state: float32 [69, 360, 512], P(None, 'lon', 'lat'), may hold values from -16 to 16
- evaluated_point_flag: int32 [360, 512], P('lon', 'lat'), may hold values 0 or 1
- parallels_each_strip: int32 [4], replicated, may hold values from 1 to 128, 361 in all
Outputs:
- parallel_quadratic_error: float32 [4, 69, 512], P(None, None, 'lat')
- parallel_systematic_error: float32 [4, 69, 512], P(None, None, 'lat')
- parallel_pattern_skill: float32 [4, 69, 512], P(None, None, 'lat')
- rmse: float32 [4, 69], replicated
- systematic_error: float32 [4, 69], replicated
- pattern_skill: float32 [4, 69], replicated
Inputs may be any that keep to these rules, and one draw needn't show every extreme that they name: `parallels_each_strip`: they sum to 361, and some band holds exactly 128 rows.
All inputs are finite; a program needn't handle non-finite values.
Results may differ from a plain program's by a relative error of at most 0.00002.
Values sent between devices are 32-bit elements.
A program may use at most 64 MiB of HBM per device.

v0:
```python
import jax
import jax.numpy as jnp
from jax import lax
from jax.sharding import PartitionSpec as P

MEAN_ROWS = 90
minimum_divisor = 0.1


def stacked_metrics(totals, horizon_tally, quantity_tally, grid_point_tally):
    block_rows = horizon_tally * quantity_tally
    width = totals.shape[1]
    error_power_two = (
        totals[:block_rows].reshape(horizon_tally, quantity_tally, width) / grid_point_tally
    )
    prediction_error = (
        totals[block_rows : 2 * block_rows].reshape(horizon_tally, quantity_tally, width)
        / grid_point_tally
    )
    paired_anomaly_term = (
        totals[2 * block_rows : 3 * block_rows].reshape(horizon_tally, quantity_tally, width)
        / grid_point_tally
    )
    predicted_spread_sum = (
        totals[3 * block_rows : 4 * block_rows].reshape(horizon_tally, quantity_tally, width)
        / grid_point_tally
    )
    observed_dispersion = (
        totals[4 * block_rows :].reshape(1, quantity_tally, width) / grid_point_tally
    )
    divisor_term = jnp.sqrt(
        jnp.maximum(predicted_spread_sum, minimum_divisor)
        * jnp.maximum(observed_dispersion, minimum_divisor)
    )
    return (error_power_two, prediction_error, paired_anomaly_term / divisor_term)


def local(
    prediction_fields, verifying_state, normal_state, evaluated_point_flag, parallels_each_strip
):
    horizon_tally, quantity_tally, zonal_circle_size, parallel_index = prediction_fields.shape
    lat_bands = lax.axis_size("lat")
    lon_spokes = lax.axis_size("lon")
    lat_total = MEAN_ROWS * lat_bands + 1
    lon_total = zonal_circle_size * lon_spokes
    band_index = lax.axis_index("lat")
    band_ids = jnp.arange(lat_bands, dtype=jnp.int32)
    first_row = jnp.sum(jnp.where(band_ids < band_index, parallels_each_strip, 0))
    band_filled = jnp.sum(jnp.where(band_ids == band_index, parallels_each_strip, 0))
    slot_ids = jnp.arange(parallel_index, dtype=jnp.int32)
    inside_band = slot_ids < band_filled
    angles = jnp.pi * jnp.arange(lat_total, dtype=jnp.float32) / (lat_total - 1)
    normalizer = jnp.sum(jnp.sin(angles))
    row_angle = jnp.pi * (first_row + slot_ids).astype(jnp.float32) / (lat_total - 1)
    area_factors = jnp.where(inside_band, jnp.sin(row_angle) * lat_total / normalizer, 0.0)
    retain_filter = (
        evaluated_point_flag.astype(jnp.float32) * inside_band.astype(jnp.float32)[None, :]
    )
    observed_anomaly = verifying_state - normal_state
    predicted_anomaly = prediction_fields - normal_state[None]
    mistake_field = predicted_anomaly - observed_anomaly[None]
    retained_entries = retain_filter[None, None]
    block_rows = horizon_tally * quantity_tally
    partial_value = jnp.concatenate(
        [
            jnp.sum(retained_entries * mistake_field * mistake_field, axis=2).reshape(
                block_rows, parallel_index
            ),
            jnp.sum(retained_entries * mistake_field, axis=2).reshape(block_rows, parallel_index),
            jnp.sum(retained_entries * predicted_anomaly * observed_anomaly[None], axis=2).reshape(
                block_rows, parallel_index
            ),
            jnp.sum(retained_entries * predicted_anomaly * predicted_anomaly, axis=2).reshape(
                block_rows, parallel_index
            ),
            jnp.sum(retain_filter[None] * observed_anomaly * observed_anomaly, axis=1),
        ],
        axis=0,
    )
    grand = lax.psum(jnp.sum(partial_value * area_factors, axis=1), ("lat", "lon"))
    zonal = lax.psum(partial_value, "lon")
    error_power_two, prediction_error, covariance_sum = stacked_metrics(
        zonal, horizon_tally, quantity_tally, float(lon_total)
    )
    total_square, total_offset, total_agree = stacked_metrics(
        grand[:, None], horizon_tally, quantity_tally, float(lat_total * lon_total)
    )
    rmse = jnp.sqrt(jnp.maximum(total_square[:, :, 0], minimum_divisor))
    return (
        error_power_two,
        prediction_error,
        covariance_sum,
        rmse,
        total_offset[:, :, 0],
        total_agree[:, :, 0],
    )


def solution(mesh):
    in_specs = (
        P(None, None, "lon", "lat"),
        P(None, "lon", "lat"),
        P(None, "lon", "lat"),
        P("lon", "lat"),
        P(),
    )
    out_specs = (P(None, None, "lat"), P(None, None, "lat"), P(None, None, "lat"), P(), P(), P())
    return jax.shard_map(local, mesh=mesh, in_specs=in_specs, out_specs=out_specs, check_vma=False)
```

profile of v0, /device:TPU:0, one launch (start us, length us, event | category | flops | bytes accessed | tf_op | source)
XLA Modules:
  0.0 119.7 jit_solution(12313264060658802673)
XLA Ops:
  7.2 0.0 copy-start.4
  7.2 0.6 sine_reduce_fusion
  7.8 1.3 %fusion.10 = (s32[]{:T(128)}, s32[]{:T(128)}) fusion(s32[4]{0:T(128)} %param.9, s32[]{:T(128)S(6)} %axis_index.15), kind=kLoop, calls=%fused_computation.33 | loop fusion | flops 22 | bytes 28 | tf_op jit(solution)/shard_map/reduce_sum | solution.py:48
  9.1 0.6 compare_convert_fusion
  9.8 0.0 copy-start
  9.8 0.0 copy-start.3
  9.8 1.9 %copy.18 = f32[69,45,128]{2,1,0:T(8,128)S(1)} copy(f32[69,45,128]{2,0,1:T(8,128)} %param.7) | data formatting | bytes 3179520 | tf_op args[2]
  11.8 0.5 copy-done.3
  12.2 0.3 fusion.3
  12.5 0.3 copy.19
  12.9 2.1 %copy-done.1 = f32[4,69,45,128]{3,0,2,1:T(4,128)S(1)} copy-done((f32[4,69,45,128]{3,0,2,1:T(4,128)S(1)}, f32[4,69,45,128]{3,0,2,1:T(4,128)}, u32[]{:S(2)}) %copy-start.1) | copy-done | bytes 6359064
  15.0 10.1 %fusion.1 = (f32[4,69,128]{2,0,1:T(4,128)S(1)}, f32[4,69,128]{2,0,1:T(4,128)S(1)}, f32[4,69,128]{2,0,1:T(4,128)S(1)}, f32[4,69,128]{2,0,1:T(4,128)S(1)}) fusion(f32[4,69,45,128]{3,0,2,1:T(4,128)S(1)} %copy-done.1, f32[69,45,128]{2,1,0:T(8,128)S(1)} %copy.19, f32[69,45,128]{2,1,0:T(8,128)S(1)} %copy.18, f32[45,128]{1,0:T(8,128)S(1)} %convert_multiply_fusion), kind=kLoop, calls=%fused_computation.5 | loop fusion | flops 17346048 | bytes 10126848 | tf_op jit(solution)/shard_map/reduce_sum | solution.py:70
  25.3 2.0 %compare_select_fusion.2 = f32[128]{0:T(128)S(1)} fusion(f32[]{:T(128)} %sine_reduce_fusion, s32[]{:T(128)} %get-tuple-element.22, s32[]{:T(128)} %get-tuple-element.23), kind=kLoop, calls=%fused_computation.30 | loop fusion | flops 896 | bytes 524 | tf_op jit(solution)/shard_map/jit(_where)/select_n | solution.py:55
  27.3 0.7 concatenate.3
  27.9 0.2 multiply_reduce_fusion.1
  28.2 0.0 all-reduce.2.cloned.1.call-start
  28.2 0.5 copy-done.2
  28.7 0.2 all-reduce.2.cloned.1.call-update
  28.9 42.2 %psum.15 = f32[1173]{0:T(1024)S(1)} all-reduce(f32[1173]{0:T(1024)S(1)} %multiply_reduce_fusion.1), channel_id=1, replica_groups=mesh['lat'=4,'lon'=8] {'lat','lon'}, use_global_device_ids=true, to_apply=%region_10.11 | all-reduce | flops 1173 | bytes 9384 | tf_op jit(solution)/shard_map/psum | solution.py:80
  71.1 0.1 fusion.6
  71.2 0.1 div.94
  71.3 0.1 max.48
  71.4 0.7 div.92
  72.0 0.7 sqrt.14
  72.7 0.1 fusion.11
  72.8 0.6 rsqrt_multiply_fusion.1
  73.4 35.3 %all-reduce.2.cloned.1.call-done = f32[1173,128]{1,0:T(8,128)} async-done(((f32[1173,128]{1,0:T(8,128)}), f32[1173,128]{1,0:T(8,128)}) %all-reduce.2.cloned.1.call-update) | async-done | bytes 600592 | tf_op jit(solution)/shard_map/psum | solution.py:81
  108.7 1.2 fusion.4
  109.9 0.8 fusion.5
  110.7 0.7 copy.26
  111.4 0.7 copy.24
  112.1 0.7 copy.25
  (18 shorter events, 0.2 us)
Async XLA Ops:
  7.2 4.6 %copy-start.4 = (s32[45,128]{1,0:T(8,128)S(1)}, s32[45,128]{1,0:T(8,128)}, u32[]{:S(2)}) copy-start(s32[45,128]{1,0:T(8,128)} %param.8) | copy-start | bytes 69124
  9.8 2.0 %copy-start = (f32[69,45,128]{2,0,1:T(8,128)S(1)}, f32[69,45,128]{2,0,1:T(8,128)}, u32[]{:S(2)}) copy-start(f32[69,45,128]{2,0,1:T(8,128)} %param.7) | copy-start | bytes 4769284
  9.8 2.4 %copy-start.3 = (f32[69,45,128]{2,0,1:T(8,128)S(1)}, f32[69,45,128]{2,0,1:T(8,128)}, u32[]{:S(2)}) copy-start(f32[69,45,128]{2,0,1:T(8,128)} %param.6) | copy-start | bytes 4769284
  12.2 2.8 %copy-start.1 = (f32[4,69,45,128]{3,0,2,1:T(4,128)S(1)}, f32[4,69,45,128]{3,0,2,1:T(4,128)}, u32[]{:S(2)}) copy-start(f32[4,69,45,128]{3,0,2,1:T(4,128)} %param.5) | copy-start | bytes 19077124
  27.9 0.8 copy-start.2
  28.2 80.5 %all-reduce.2.cloned.1.call-start = ((), (), s32[]{:S(2)}) async-start(), calls=%async_computation | async-start | bytes 1204224 | tf_op jit(solution)/shard_map/psum | solution.py:81
Sparse Core Ops, SparseCore 0:
  32.4 76.1 all-reduce.1
where the time goes:
time: 120 us
  blocking collectives  42.2 us (35%)
  waiting for transfers between devices  35.5 us (30%)
  other arithmetic  18 us (15%)
  between operations  14.2 us (12%)
  local copies, waits for them, and re-layouts  9.77 us (8%)
    psum x1, blocking collectives, local(): lax.psum(jnp.sum(partial_value * area_factors, axis=1), ('lat', 'lon'))  42.2 us
    psum x1, waiting for transfers between devices, local(): zonal = lax.psum(partial_value, 'lon')  35.3 us
    reduce_sum x1, other arithmetic, local(): jnp.sum(retained_entries * predicted_anomaly * observed_anomaly[None], ax...  10.1 us
    unnamed x14, local copies, waits for them, and re-layouts  7.14 us
  transfers between devices with their start and end apart: 1, of which 1 were waited for; matrix products, arithmetic and copies ran while one was open for 2% of the time, Pallas kernels for 0%

commit v1 on v0

--- a/solution.py
+++ b/solution.py
@@ -2,6 +2,7 @@
 import jax.numpy as jnp
 from jax import lax
 from jax.sharding import PartitionSpec as P
+from jax.lax import psum
 
 MEAN_ROWS = 90
 minimum_divisor = 0.1
@@ -77,7 +78,9 @@
         ],
         axis=0,
     )
-    grand = lax.psum(jnp.sum(partial_value * area_factors, axis=1), ("lat", "lon"))
+    grand = jnp.sum(partial_value * area_factors, axis=1)
+    for m in ("lon", "lat"):
+        grand = psum(grand, m)
     zonal = lax.psum(partial_value, "lon")
     error_power_two, prediction_error, covariance_sum = stacked_metrics(
         zonal, horizon_tally, quantity_tally, float(lon_total)

time: 120 us -> 120 us (level)
  blocking collectives: 42.2 us -> 29.2 us
  waiting for transfers between devices: 35.5 us -> 48.5 us
    psum x1, waiting for transfers between devices: 35.3 us -> 48.4 us  [local(): zonal = lax.psum(partial_value, 'lon')]
    psum x1 -> x2, blocking collectives: 42.2 us -> 29.2 us  [local(): grand = psum(grand, m)]
where the time goes in v1:
time: 120 us
  waiting for transfers between devices  48.5 us (40%)
  blocking collectives  29.2 us (24%)
  other arithmetic  18 us (15%)
  between operations  14.2 us (12%)
  local copies, waits for them, and re-layouts  9.77 us (8%)
    psum x1, waiting for transfers between devices, local(): zonal = lax.psum(partial_value, 'lon')  48.4 us
    psum x2, blocking collectives, local(): grand = psum(grand, m)  29.2 us
    reduce_sum x1, other arithmetic, local(): jnp.sum(retained_entries * predicted_anomaly * observed_anomaly[None], ax...  10.1 us
    unnamed x14, local copies, waits for them, and re-layouts  7.14 us
  transfers between devices with their start and end apart: 1, of which 1 were waited for; matrix products, arithmetic and copies ran while one was open for 2% of the time, Pallas kernels for 0%

profile of v1, /device:TPU:0, one launch (start us, length us, event | category | flops | bytes accessed | tf_op | source)
XLA Modules:
  0.0 119.7 jit_solution(7372593002769524436)
XLA Ops:
  7.2 0.6 sine_reduce_fusion
  7.8 1.3 %fusion.10 = (s32[]{:T(128)}, s32[]{:T(128)}) fusion(s32[4]{0:T(128)} %param.9, s32[]{:T(128)S(6)} %axis_index.15), kind=kLoop, calls=%fused_computation.33 | loop fusion | flops 22 | bytes 28 | tf_op jit(solution)/shard_map/reduce_sum | solution.py:49
  9.1 0.6 compare_convert_fusion
  9.8 0.0 copy-start
  9.8 0.0 copy-start.3
  9.8 1.9 %copy.18 = f32[69,45,128]{2,1,0:T(8,128)S(1)} copy(f32[69,45,128]{2,0,1:T(8,128)} %param.7) | data formatting | bytes 3179520 | tf_op args[2]
  11.8 0.5 copy-done.3
  12.2 0.3 fusion.3
  12.5 0.3 copy.19
  12.9 2.1 %copy-done.1 = f32[4,69,45,128]{3,0,2,1:T(4,128)S(1)} copy-done((f32[4,69,45,128]{3,0,2,1:T(4,128)S(1)}, f32[4,69,45,128]{3,0,2,1:T(4,128)}, u32[]{:S(2)}) %copy-start.1) | copy-done | bytes 6359064
  15.0 10.1 %fusion.1 = (f32[4,69,128]{2,0,1:T(4,128)S(1)}, f32[4,69,128]{2,0,1:T(4,128)S(1)}, f32[4,69,128]{2,0,1:T(4,128)S(1)}, f32[4,69,128]{2,0,1:T(4,128)S(1)}) fusion(f32[4,69,45,128]{3,0,2,1:T(4,128)S(1)} %copy-done.1, f32[69,45,128]{2,1,0:T(8,128)S(1)} %copy.19, f32[69,45,128]{2,1,0:T(8,128)S(1)} %copy.18, f32[45,128]{1,0:T(8,128)S(1)} %convert_multiply_fusion), kind=kLoop, calls=%fused_computation.5 | loop fusion | flops 17346048 | bytes 10126848 | tf_op jit(solution)/shard_map/reduce_sum | solution.py:71
  25.3 2.0 %compare_select_fusion.2 = f32[128]{0:T(128)S(1)} fusion(f32[]{:T(128)} %sine_reduce_fusion, s32[]{:T(128)} %get-tuple-element.22, s32[]{:T(128)} %get-tuple-element.23), kind=kLoop, calls=%fused_computation.30 | loop fusion | flops 896 | bytes 524 | tf_op jit(solution)/shard_map/jit(_where)/select_n | solution.py:56
  27.3 0.7 concatenate.3
  27.9 0.2 multiply_reduce_fusion.1
  28.2 0.0 all-reduce.2.cloned.1.call-start
  28.2 0.5 copy-done.2
  28.7 0.2 all-reduce.2.cloned.1.call-update
  28.9 23.4 %psum.22 = f32[1173]{0:T(1024)S(1)} all-reduce(f32[1173]{0:T(1024)S(1)} %multiply_reduce_fusion.1), channel_id=1, replica_groups=mesh['lat'=4,'lon'=8] {'lon'}, use_global_device_ids=true, to_apply=%region_10.11 | all-reduce | flops 1173 | bytes 9384 | tf_op jit(solution)/shard_map/psum | solution.py:83
  52.4 5.8 %psum.23 = f32[1173]{0:T(1024)S(1)} all-reduce(f32[1173]{0:T(1024)S(1)} %psum.22), channel_id=1, replica_groups=mesh['lat'=4,'lon'=8] {'lat'}, use_global_device_ids=true, to_apply=%region_11.12 | all-reduce | flops 1173 | bytes 9384 | tf_op jit(solution)/shard_map/psum | solution.py:83
  58.1 0.1 fusion.6
  58.2 0.1 div.94
  58.3 0.1 max.48
  58.4 0.7 div.92
  59.1 0.7 sqrt.14
  59.7 0.1 fusion.11
  59.8 0.6 rsqrt_multiply_fusion.1
  60.4 48.4 %all-reduce.2.cloned.1.call-done = f32[1173,128]{1,0:T(8,128)} async-done(((f32[1173,128]{1,0:T(8,128)}), f32[1173,128]{1,0:T(8,128)}) %all-reduce.2.cloned.1.call-update) | async-done | bytes 600592 | tf_op jit(solution)/shard_map/psum | solution.py:84
  108.7 1.2 fusion.4
  110.0 0.8 fusion.5
  110.8 0.7 copy.26
  111.5 0.7 copy.24
  112.2 0.7 copy.25
  (19 shorter events, 0.2 us)
Async XLA Ops:
  7.2 4.6 %copy-start.4 = (s32[45,128]{1,0:T(8,128)S(1)}, s32[45,128]{1,0:T(8,128)}, u32[]{:S(2)}) copy-start(s32[45,128]{1,0:T(8,128)} %param.8) | copy-start | bytes 69124
  9.8 2.0 %copy-start = (f32[69,45,128]{2,0,1:T(8,128)S(1)}, f32[69,45,128]{2,0,1:T(8,128)}, u32[]{:S(2)}) copy-start(f32[69,45,128]{2,0,1:T(8,128)} %param.7) | copy-start | bytes 4769284
  9.8 2.4 %copy-start.3 = (f32[69,45,128]{2,0,1:T(8,128)S(1)}, f32[69,45,128]{2,0,1:T(8,128)}, u32[]{:S(2)}) copy-start(f32[69,45,128]{2,0,1:T(8,128)} %param.6) | copy-start | bytes 4769284
  12.2 2.8 %copy-start.1 = (f32[4,69,45,128]{3,0,2,1:T(4,128)S(1)}, f32[4,69,45,128]{3,0,2,1:T(4,128)}, u32[]{:S(2)}) copy-start(f32[4,69,45,128]{3,0,2,1:T(4,128)} %param.5) | copy-start | bytes 19077124
  27.9 0.8 copy-start.2
  28.2 80.5 %all-reduce.2.cloned.1.call-start = ((), (), s32[]{:S(2)}) async-start(), calls=%async_computation | async-start | bytes 1204224 | tf_op jit(solution)/shard_map/psum | solution.py:84
Sparse Core Ops, SparseCore 0:
  32.4 76.2 all-reduce.1
